TPU v7x, 32 devices: a whole 2x2x4 slice. The times are simulated.
32 devices in a mesh: band: 16 (over z, y, core), chan: 2 (over x).
Axes of the slice: x: 2, y: 2, z: 4, core: 2. Of those that a mesh axis runs over, the one named last changes fastest.
Arguments:
- fine_features: bfloat16 [2, 192, 128, 512], P(None, 'chan', 'band'), may hold values from -100 to 100
- coarse_level: bfloat16 [2, 256, 64, 256], P(None, 'chan', 'band'), may hold values from -100 to 100
- lat_weight: bfloat16 [256, 192], P('chan'), may hold values from -0.4375 to 0.4375
- lat_gain: bfloat16 [256], P('chan'), may hold values from 0.099609375 to 1.8984375
- lat_shift: bfloat16 [256], P('chan'), may hold values from -3 to 3
- out_weight: bfloat16 [3, 3, 256, 256], P(None, None, 'chan'), may hold values from -0.125 to 0.125
- out_gain: bfloat16 [256], P('chan'), may hold values from 0.099609375 to 1.8984375
- out_shift: bfloat16 [256], P('chan'), may hold values from -3 to 3
- mask_weight: bfloat16 [256, 256], P('chan'), may hold values from -0.375 to 0.375
- mask_bias: bfloat16 [256], P('chan'), may hold values from -1.796875 to 1.796875
- queries: bfloat16 [200, 256], replicated, may hold values from -128 to 128
Outputs:
- log_probs: float32 [2, 200, 128, 512], P(None, None, ('band', 'chan'))
All inputs are finite; a program needn't handle non-finite values.
Results may differ from a plain program's by a relative error of at most 0.0058.
Values may be sent and summed in bfloat16 or wider, within the bound.
A program may use at most 128 MiB of HBM per device.

v0:
```python
import jax
import jax.numpy as jnp
from jax import lax
from jax.sharding import PartitionSpec as P

D = 256
GROUPS = 32
epsilon = 1e-05


def extended_2(cells, sides, width):
    for axis, dim in sides:
        count = lax.axis_size(axis)
        ends = count - 1
        head = lax.slice_in_dim(cells, 0, width, axis=dim)
        tail = lax.slice_in_dim(cells, cells.shape[dim] - width, cells.shape[dim], axis=dim)
        cells = jnp.concatenate(
            [
                lax.ppermute(tail, axis, [(i, (i + 1) % count) for i in range(ends)]),
                cells,
                lax.ppermute(head, axis, [((i + 1) % count, i) for i in range(ends)]),
            ],
            axis=dim,
        )
    return cells


def interp(padded, axis):
    length = padded.shape[axis] - 2
    before = lax.slice_in_dim(padded, 0, length, axis=axis)
    middle = lax.slice_in_dim(padded, 1, length + 1, axis=axis)
    after = lax.slice_in_dim(padded, 2, length + 2, axis=axis)
    even_part = 0.25 * before + 0.75 * middle
    odd_part = 0.75 * middle + 0.25 * after
    paired = jnp.stack([even_part, odd_part], axis + 1)
    new_shape = list(middle.shape)
    new_shape[axis] = 2 * length
    return paired.reshape(new_shape)


def conv_taps(taps_weight, padded, row_count, col_count):
    summed = None
    for row_tap in range(3):
        for col_tap in range(3):
            window = padded[:, :, row_tap : row_tap + row_count, col_tap : col_tap + col_count]
            term = jnp.einsum(
                "oc,ncrw->norw",
                taps_weight[row_tap, col_tap],
                window,
                preferred_element_type=jnp.float32,
            )
            summed = term if summed is None else summed + term
    return summed


def apply_norm(blocks, mean_value, variance, full_shape, gain, shift):
    scaled = (
        (blocks - mean_value[:, :, None]) * lax.rsqrt(variance[:, :, None] + epsilon)
    ).reshape(full_shape)
    return (
        scaled * gain.astype(jnp.float32)[None, :, None, None]
        + shift.astype(jnp.float32)[None, :, None, None]
    )


def per_device(
    fine_features,
    coarse_level,
    lat_weight,
    lat_gain,
    lat_shift,
    out_weight,
    out_gain,
    out_shift,
    mask_weight,
    mask_bias,
    queries,
):
    images, in_share, band_rows, columns = fine_features.shape
    out_share = lat_weight.shape[0]
    group_size = D // GROUPS
    band_count = lax.axis_size("band")
    pixel_count = float(group_size * band_rows * band_count * columns)
    lateral = jnp.einsum(
        "oc,ncrw->norw",
        lat_weight,
        lax.all_gather(fine_features, "chan", axis=1, tiled=True),
        preferred_element_type=jnp.float32,
    )
    lat_blocks = lateral.reshape(images, out_share // group_size, -1)
    lat_mean = lax.psum(jnp.sum(lat_blocks, 2), "band") / pixel_count
    deviation = lat_blocks - lat_mean[:, :, None]
    lat_var = lax.psum(jnp.sum(deviation * deviation, 2), "band") / pixel_count
    lat_normed = apply_norm(lat_blocks, lat_mean, lat_var, lateral.shape, lat_gain, lat_shift)
    band_index = lax.axis_index("band")
    extended = extended_2(coarse_level, (("band", 2),), 1)
    top_row = jnp.where(band_index == 0, extended[:, :, 1:2], extended[:, :, 0:1])
    bottom_row = jnp.where(band_index == band_count - 1, extended[:, :, -2:-1], extended[:, :, -1:])
    extended = jnp.concatenate([top_row, extended[:, :, 1:-1], bottom_row], 2).astype(jnp.float32)
    extended = jnp.pad(extended, ((0, 0), (0, 0), (0, 0), (1, 1)), mode="edge")
    upsampled = interp(interp(extended, 2), 3)
    joined = (lat_normed + upsampled).astype(jnp.bfloat16)
    row_joined = lax.all_to_all(joined, "chan", split_axis=2, concat_axis=1, tiled=True)
    conv_weight, full_gain, full_shift, full_mask, full_bias = (
        lax.all_gather(out_weight, "chan", axis=2, tiled=True),
        lax.all_gather(out_gain, "chan", axis=0, tiled=True),
        lax.all_gather(out_shift, "chan", axis=0, tiled=True),
        lax.all_gather(mask_weight, "chan", axis=0, tiled=True),
        lax.all_gather(mask_bias, "chan", axis=0, tiled=True),
    )
    row_count = row_joined.shape[2]
    padded = extended_2(row_joined, ((("band", "chan"), 2),), 1)
    padded = jnp.pad(padded, ((0, 0), (0, 0), (0, 0), (1, 1)))
    conv_out = conv_taps(conv_weight, padded, row_count, columns)
    local_groups = conv_out.shape[1] // group_size
    conv_blocks = conv_out.reshape(images, local_groups, -1)
    out_mean = lax.psum(jnp.sum(conv_blocks, 2), ("band", "chan")) / pixel_count
    deviation = conv_blocks - out_mean[:, :, None]
    out_var = lax.psum(jnp.sum(deviation * deviation, 2), ("band", "chan")) / pixel_count
    activated = jnp.maximum(
        apply_norm(conv_blocks, out_mean, out_var, conv_out.shape, full_gain, full_shift), 0.0
    ).astype(jnp.bfloat16)
    mixed = jnp.einsum("oc,ncrw->norw", full_mask, activated, preferred_element_type=jnp.float32)
    features = (mixed + full_bias.astype(jnp.float32)[None, :, None, None]).astype(jnp.bfloat16)
    logits = jnp.einsum("qc,ncrw->nqrw", queries, features, preferred_element_type=jnp.float32)
    peak = jnp.max(logits, axis=1, keepdims=True)
    shifted = logits - peak
    return shifted - jnp.log(jnp.sum(jnp.exp(shifted), axis=1, keepdims=True))


def solution(mesh):
    return jax.shard_map(
        per_device,
        mesh=mesh,
        in_specs=(
            P(None, "chan", "band", None),
            P(None, "chan", "band", None),
            P("chan", None),
            P("chan"),
            P("chan"),
            P(None, None, "chan", None),
            P("chan"),
            P("chan"),
            P("chan", None),
            P("chan"),
            P(),
        ),
        out_specs=P(None, None, ("band", "chan"), None),
        check_vma=False,
    )
```

profile of v0, /device:TPU:0, one launch (start us, length us, event | category | flops | bytes accessed | tf_op | source)
XLA Modules:
  0.0 355.2 jit_solution(3142790244294858030)
XLA Ops:
  6.6 3.1 copy.21
  9.8 0.4 fusion.60
  10.1 2.4 collective-permute-start
  12.6 1.3 collective-permute-start.1
  13.9 4.2 %collective-permute-done.1 = bf16[2,128,1,256]{3,2,1,0:T(2,128)(2,1)S(1)} collective-permute-done((bf16[2,128,1,256]{3,2,1,0:T(2,128)(2,1)S(1)}, bf16[2,128,1,256]{3,2,1,0:T(2,128)(2,1)S(1)}, u32[]{:S(2)}, u32[]{:S(2)}) %collective-permute-start.1) | collective-permute-done | bytes 131104 | tf_op jit(solution)/shard_map/ppermute | solution.py:21
  18.1 0.8 broadcast_select_fusion.1
  18.9 0.8 maximum_convert_fusion.6
  19.7 0.3 fusion.59
  20.1 1.1 pad_maximum_fusion.1
  21.2 1.0 fusion.43
  22.2 2.4 pad_maximum_fusion.2
  24.6 3.2 copy.22
  27.9 0.6 fusion.32
  28.5 0.3 pad_maximum_fusion
  28.8 5.2 %copy.23 = f32[2,128,8,256,2]{1,4,3,2,0:T(2,128)} copy(f32[2,128,8,256,2]{1,3,2,0,4:T(8,128)S(1)} %pad_maximum_fusion) | data formatting | bytes 8388608 | tf_op jit(solution)/shard_map/stack | solution.py:35
  34.0 23.6 %all-gather.6.cloned.1.call-done = bf16[2,192,8,512]{3,1,2,0:T(8,128)(2,1)} async-done(((bf16[2,96,8,512]{3,1,2,0:T(8,128)(2,1)}), bf16[2,192,8,512]{3,1,2,0:T(8,128)(2,1)}) %all-gather.6.cloned.1.call-update) | async-done | bytes 3145744 | tf_op jit(solution)/shard_map/all_gather | solution.py:87
  57.5 5.4 %bitcast_reduce_fusion.1 = (f32[2,128]{1,0:T(2,128)S(1)}, f32[2,8,512,128]{3,2,1,0:T(8,128)}) fusion(bf16[2,192,8,512]{3,1,2,0:T(8,128)(2,1)} %all-gather.6.cloned.1.call-done, bf16[128,192]{0,1:T(8,128)(2,1)S(1)} %copy-done.5), kind=kOutput, calls=%fused_computation.7 | convolution fusion | flops 403701504 | bytes 7390208 | tf_op jit(solution)/shard_map/oc,ncrw->norw/dot_general | solution.py:84
  62.9 0.1 reduce_sum.55
  63.0 0.1 reduce_sum.59
  63.1 33.2 %psum.28 = f32[2,16]{1,0:T(2,128)S(1)} all-reduce(f32[2,16]{1,0:T(2,128)S(1)} %reduce_sum.59), channel_id=1, replica_groups=mesh['band'=16,'chan'=2] {'band'}, use_global_device_ids=true, to_apply=%region_2.0 | all-reduce | flops 32 | bytes 256 | tf_op jit(solution)/shard_map/psum | solution.py:91
  96.4 0.1 sub.53
  96.5 2.8 multiply_reduce_fusion.1
  99.3 0.1 reduce_sum.62
  99.4 29.5 %psum.29 = f32[2,16]{1,0:T(2,128)S(1)} all-reduce(f32[2,16]{1,0:T(2,128)S(1)} %reduce_sum.62), channel_id=1, replica_groups=mesh['band'=16,'chan'=2] {'band'}, use_global_device_ids=true, to_apply=%region_5.6 | all-reduce | flops 32 | bytes 256 | tf_op jit(solution)/shard_map/psum | solution.py:93
  128.9 0.1 mul.72
  129.0 4.3 %add_convert_fusion.1 = bf16[2,128,8,512]{1,3,2,0:T(8,128)(2,1)S(1)} fusion(f32[2,128,8,512]{1,3,2,0:T(8,128)} %bitcast.138, f32[2,8,512,128]{3,2,1,0:T(8,128)} %get-tuple-element.18, f32[128]{0:T(128)S(1)} %convert_element_type.33, f32[128]{0:T(128)S(1)} %convert_element_type.32, f32[2,128]{1,0:T(2,128)S(1)} %mul.72, f32[2,128]{1,0:T(2,128)S(1)} %sub.53), kind=kLoop, calls=%fused_computation.12 | loop fusion | flops 6291456 | bytes 10488832 | tf_op jit(solution)/shard_map/convert_element_type | solution.py:102
  133.4 1.5 copy.24
  134.9 3.8 %all-to-all-start = ((bf16[2,128,8,512]{1,3,0,2:T(8,128)(2,1)}), bf16[2,128,8,512]{1,3,0,2:T(8,128)(2,1)S(1)}, u32[]{:S(2)}, u32[]{:S(2)}) async-start(bf16[2,128,8,512]{1,3,0,2:T(8,128)(2,1)} %copy.24), calls=%async_computation | async-start | bytes 4194304 | tf_op jit(solution)/shard_map/all_to_all | solution.py:103
  138.7 0.7 all-gather.8.cloned.1.call-update
  139.4 37.0 %all-to-all-done = bf16[2,128,8,512]{1,3,0,2:T(8,128)(2,1)S(1)} async-done(((bf16[2,128,8,512]{1,3,0,2:T(8,128)(2,1)}), bf16[2,128,8,512]{1,3,0,2:T(8,128)(2,1)S(1)}, u32[]{:S(2)}, u32[]{:S(2)}) %all-to-all-start) | async-done | bytes 2097184 | tf_op jit(solution)/shard_map/all_to_all | solution.py:103
  176.4 3.5 copy.42
  179.9 3.2 all_to_all.16
  183.1 1.1 fusion.58
  184.2 2.2 collective-permute-start.2
  186.4 11.5 %all-gather = bf16[2,1,128]{2,1,0:T(2,128)(2,1)S(1)} all-gather(bf16[1,1,128]{2,1,0:T(2,128)(2,1)S(1)} %bitcast.144), channel_id=1, replica_groups=mesh['band'=16,'chan'=2] {'chan'}, dimensions={0}, use_global_device_ids=true | all-gather | bytes 768 | tf_op jit(solution)/shard_map/all_gather | solution.py:106
  198.0 4.2 %all-gather.1 = bf16[2,1,128]{2,1,0:T(2,128)(2,1)S(1)} all-gather(bf16[1,1,128]{2,1,0:T(2,128)(2,1)S(1)} %bitcast.145), channel_id=1, replica_groups=mesh['band'=16,'chan'=2] {'chan'}, dimensions={0}, use_global_device_ids=true | all-gather | bytes 768 | tf_op jit(solution)/shard_map/all_gather | solution.py:107
  202.2 4.2 %all-gather.2 = bf16[2,1,128]{2,1,0:T(2,128)(2,1)S(1)} all-gather(bf16[1,1,128]{2,1,0:T(2,128)(2,1)S(1)} %bitcast.146), channel_id=1, replica_groups=mesh['band'=16,'chan'=2] {'chan'}, dimensions={0}, use_global_device_ids=true | all-gather | bytes 768 | tf_op jit(solution)/shard_map/all_gather | solution.py:109
  206.4 4.9 %all_gather.22 = bf16[256,256]{1,0:T(8,128)(2,1)S(1)} all-gather(bf16[128,256]{1,0:T(8,128)(2,1)S(1)} %copy-done.4), channel_id=1, replica_groups=mesh['band'=16,'chan'=2] {'chan'}, dimensions={0}, use_global_device_ids=true | all-gather | bytes 196608 | tf_op jit(solution)/shard_map/all_gather | solution.py:108
  211.4 1.3 collective-permute-start.3
  212.7 1.7 fusion.44
  214.5 2.7 fusion.7
  217.2 9.8 %collective-permute-done.3 = bf16[2,256,1,512]{1,3,2,0:T(8,128)(2,1)S(1)} collective-permute-done((bf16[2,256,1,512]{1,3,2,0:T(8,128)(2,1)}, bf16[2,256,1,512]{1,3,2,0:T(8,128)(2,1)S(1)}, u32[]{:S(2)}, u32[]{:S(2)}) %collective-permute-start.3) | collective-permute-done | bytes 524320 | tf_op jit(solution)/shard_map/ppermute | solution.py:21
  226.9 1.0 fusion.6
  227.9 2.7 fusion.11
  230.6 2.7 fusion.19
  233.3 2.7 fusion.21
  236.0 2.7 fusion.23
  238.7 2.7 fusion.25
  241.5 2.8 fusion.27
  244.2 0.7 copy-done.1
  244.9 11.3 %bitcast_reduce_fusion = (f32[2,256]{1,0:T(2,128)S(1)}, f32[2,4,512,256]{3,2,1,0:T(8,128)}) fusion(bf16[3,3,256,256]{3,2,1,0:T(8,128)(2,1)} %all-gather.8.cloned.1.call-done, bf16[2,256,6,514]{1,3,2,0:T(8,128)(2,1)S(1)} %fusion.6, f32[2,4,512,256]{3,2,1,0:T(8,128)} %fusion.11, f32[2,4,512,256]{3,2,1,0:T(8,128)} %fusion.19, f32[2,4,512,256]{3,2,1,0:T(8,128)} %fusion.21, ...), kind=kOutput, calls=%fused_computation.5 | convolution fusion | flops 546307584 | bytes 39979008 | tf_op jit(solution)/shard_map/oc,ncrw->norw/dot_general | solution.py:46
  256.2 0.1 reduce_sum.80
  256.3 0.1 reduce_sum.81
  256.4 37.0 %psum.30 = f32[2,32]{1,0:T(2,128)S(1)} all-reduce(f32[2,32]{1,0:T(2,128)S(1)} %reduce_sum.81), channel_id=1, replica_groups=mesh['band'=16,'chan'=2] {'band','chan'}, use_global_device_ids=true, to_apply=%region_8.9 | all-reduce | flops 64 | bytes 512 | tf_op jit(solution)/shard_map/psum | solution.py:117
  293.5 0.1 sub.57
  293.6 2.7 multiply_reduce_fusion
  296.2 0.1 reduce_sum.83
  296.3 0.1 reduce_sum.84
  296.4 40.9 %psum.31 = f32[2,32]{1,0:T(2,128)S(1)} all-reduce(f32[2,32]{1,0:T(2,128)S(1)} %reduce_sum.84), channel_id=1, replica_groups=mesh['band'=16,'chan'=2] {'band','chan'}, use_global_device_ids=true, to_apply=%region_11.12 | all-reduce | flops 64 | bytes 512 | tf_op jit(solution)/shard_map/psum | solution.py:119
  337.4 0.1 mul.85
  337.5 3.7 %fusion.33 = f32[2,4,512,200]{2,3,1,0:T(8,128)S(1)} fusion(f32[2,4,512,256]{3,2,1,0:T(8,128)} %get-tuple-element.20, f32[256]{0:T(256)S(1)} %bitcast.143, f32[256]{0:T(256)S(1)} %bitcast.142, f32[256]{0:T(256)S(1)} %bitcast.141, f32[2,256]{1,0:T(2,128)S(1)} %mul.85, f32[2,256]{1,0:T(2,128)S(1)} %sub.57, bf16[256,256]{1,0:T(8,128)(2,1)S(1)} %all_gather.22, ...), kind=kOutput, calls=%fused_computation.52 | convolution fusion | flops 964689920 | bytes 7711744 | tf_op jit(solution)/shard_map/qc,ncrw->nqrw/dot_general | solution.py:125
  341.2 2.9 exponential_reduce_fusion
  344.1 0.4 log_subtract_fusion
  344.6 3.8 %copy.27 = f32[2,200,4,512]{3,2,1,0:T(4,128)} copy(f32[2,200,4,512]{3,1,2,0:T(8,128)S(1)} %log_subtract_fusion) | data formatting | bytes 6553600 | tf_op jit(solution)/shard_map/sub | solution.py:128
  (41 shorter events, 0.6 us)
Async XLA Ops:
  6.5 331.0 %copy-start = (bf16[200,256]{1,0:T(8,128)(2,1)S(1)}, bf16[200,256]{1,0:T(8,128)(2,1)}, u32[]{:S(2)}) copy-start(bf16[200,256]{1,0:T(8,128)(2,1)} %param.21) | copy-start | bytes 307204
  6.5 3.2 copy-start.2
  6.5 7.3 %copy-start.6 = (bf16[128]{0:T(256)(128)(2,1)S(1)}, bf16[128]{0:T(256)(128)(2,1)}, u32[]{:S(2)}) copy-start(bf16[128]{0:T(256)(128)(2,1)} %param.14) | copy-start | bytes 772
  6.5 7.3 %copy-start.7 = (bf16[128]{0:T(256)(128)(2,1)S(1)}, bf16[128]{0:T(256)(128)(2,1)}, u32[]{:S(2)}) copy-start(bf16[128]{0:T(256)(128)(2,1)} %param.15) | copy-start | bytes 772
  6.5 51.0 %all-gather.6.cloned.1.call-start = ((), (), s32[]{:S(2)}) async-start(), calls=%async_computation.1 | async-start | bytes 4718592 | tf_op jit(solution)/shard_map/all_gather | solution.py:87
  10.1 3.8 %collective-permute-start = (bf16[2,128,1,256]{3,2,1,0:T(2,128)(2,1)S(1)}, bf16[2,128,1,256]{3,2,1,0:T(2,128)(2,1)S(1)}, u32[]{:S(2)}, u32[]{:S(2)}) collective-permute-start(bf16[2,128,1,256]{3,2,1,0:T(2,128)(2,1)S(1)} %get-tuple-element.15), channel_id=1, source_target_pairs={{0,2},{2,4},{4,6},{6,8},{8,10},{10,12},{12,14},{14,16},{16,18},{18... | collective-permute-start | bytes 393224 | tf_op jit(solution)/shard_map/ppermute | solution.py:19
  12.6 5.5 %collective-permute-start.1 = (bf16[2,128,1,256]{3,2,1,0:T(2,128)(2,1)S(1)}, bf16[2,128,1,256]{3,2,1,0:T(2,128)(2,1)S(1)}, u32[]{:S(2)}, u32[]{:S(2)}) collective-permute-start(bf16[2,128,1,256]{3,2,1,0:T(2,128)(2,1)S(1)} %get-tuple-element.16), channel_id=1, source_target_pairs={{2,0},{4,2},{6,4},{8,6},{10,8},{12,10},{14,12},{16,14},{18,16},{20... | collective-permute-start | bytes 393224 | tf_op jit(solution)/shard_map/ppermute | solution.py:21
  28.8 28.8 %copy-start.5 = (bf16[128,192]{0,1:T(8,128)(2,1)S(1)}, bf16[128,192]{0,1:T(8,128)(2,1)}, u32[]{:S(2)}) copy-start(bf16[128,192]{0,1:T(8,128)(2,1)} %param.13) | copy-start | bytes 147460
  134.9 41.5 %all-to-all-start = ((bf16[2,128,8,512]{1,3,0,2:T(8,128)(2,1)}), bf16[2,128,8,512]{1,3,0,2:T(8,128)(2,1)S(1)}, u32[]{:S(2)}, u32[]{:S(2)}) async-start(bf16[2,128,8,512]{1,3,0,2:T(8,128)(2,1)} %copy.24), calls=%async_computation | async-start | bytes 4194304 | tf_op jit(solution)/shard_map/all_to_all | solution.py:103
  138.6 74.0 %all-gather.8.cloned.1.call-start = ((), (), s32[]{:S(2)}) async-start(), calls=%async_computation.2 | async-start | bytes 1769472 | tf_op jit(solution)/shard_map/all_gather | solution.py:105
  179.9 6.5 %copy-start.8 = (bf16[128]{0:T(256)(128)(2,1)S(1)}, bf16[128]{0:T(256)(128)(2,1)}, u32[]{:S(2)}) copy-start(bf16[128]{0:T(256)(128)(2,1)} %param.17) | copy-start | bytes 772
  179.9 18.1 %copy-start.9 = (bf16[128]{0:T(256)(128)(2,1)S(1)}, bf16[128]{0:T(256)(128)(2,1)}, u32[]{:S(2)}) copy-start(bf16[128]{0:T(256)(128)(2,1)} %param.18) | copy-start | bytes 772
  179.9 22.3 %copy-start.10 = (bf16[128]{0:T(256)(128)(2,1)S(1)}, bf16[128]{0:T(256)(128)(2,1)}, u32[]{:S(2)}) copy-start(bf16[128]{0:T(256)(128)(2,1)} %param.20) | copy-start | bytes 772
  179.9 26.6 %copy-start.4 = (bf16[128,256]{1,0:T(8,128)(2,1)S(1)}, bf16[128,256]{1,0:T(8,128)(2,1)}, u32[]{:S(2)}) copy-start(bf16[128,256]{1,0:T(8,128)(2,1)} %param.19) | copy-start | bytes 196612
  184.2 30.2 %collective-permute-start.2 = (bf16[2,256,1,512]{1,3,2,0:T(8,128)(2,1)}, bf16[2,256,1,512]{1,3,2,0:T(8,128)(2,1)S(1)}, u32[]{:S(2)}, u32[]{:S(2)}) collective-permute-start(bf16[2,256,1,512]{1,3,2,0:T(8,128)(2,1)} %get-tuple-element.9), channel_id=1, source_target_pairs={{0,1},{1,2},{2,3},{3,4},{4,5},{5,6},{6,7},{7,8},{8,9},{9,10},{10,1... | collective-permute-start | bytes 1572872 | tf_op jit(solution)/shard_map/ppermute | solution.py:19
  211.4 15.6 %collective-permute-start.3 = (bf16[2,256,1,512]{1,3,2,0:T(8,128)(2,1)}, bf16[2,256,1,512]{1,3,2,0:T(8,128)(2,1)S(1)}, u32[]{:S(2)}, u32[]{:S(2)}) collective-permute-start(bf16[2,256,1,512]{1,3,2,0:T(8,128)(2,1)} %get-tuple-element.10), channel_id=1, source_target_pairs={{1,0},{2,1},{3,2},{4,3},{5,4},{6,5},{7,6},{8,7},{9,8},{10,9},{11,1... | collective-permute-start | bytes 1572872 | tf_op jit(solution)/shard_map/ppermute | solution.py:21
  212.7 1.8 copy-start.3
  241.5 3.4 copy-start.1
Sparse Core Ops, SparseCore 0:
  9.9 47.6 all-gather.5
  141.0 33.2 all-gather.7
where the time goes:
time: 356 us; the launch traced here: 355 us
  blocking collectives  166 us (47%)
  waiting for transfers between devices  75.2 us (21%)
  matrix products  41.1 us (12%)
  local copies, waits for them, and re-layouts  27.1 us (8%)
  other arithmetic  21.5 us (6%)
  between operations  13.7 us (4%)
  starting transfers between devices  11 us (3%)
    psum x1, blocking collectives, per_device(): lax.psum(jnp.sum(deviation * deviation, 2), ('band', 'chan')) / pixel_count  40.9 us
    psum x1, blocking collectives, per_device(): out_mean = lax.psum(jnp.sum(conv_blocks, 2), ('band', 'chan')) / pixel_count  37 us
    all_to_all x1, waiting for transfers between devices, per_device(): lax.all_to_all(joined, 'chan', split_axis=2, concat_axis=1, tiled=True)  37 us
    psum x1, blocking collectives, per_device(): lat_mean = lax.psum(jnp.sum(lat_blocks, 2), 'band') / pixel_count  33.2 us
    dot_general x9, matrix products, conv_taps(): jnp.einsum('oc,ncrw->norw', taps_weight[row_tap, col_tap], window, prefer...  32.1 us
    psum x1, blocking collectives, per_device(): lat_var = lax.psum(jnp.sum(deviation * deviation, 2), 'band') / pixel_count  29.5 us
    all_gather x1, waiting for transfers between devices, per_device(): lax.all_gather(fine_features, 'chan', axis=1, tiled=True)  23.6 us
    ppermute x2, waiting for transfers between devices, extended_2(): lax.ppermute(head, axis, [((i + 1) % count, i) for i in range(ends)])  13.9 us
  transfers between devices with their start and end apart: 7, of which 4 were waited for; matrix products, arithmetic and copies ran while one was open for 7% of the time, Pallas kernels for 0%

commit v1 on v0

--- a/solution.py
+++ b/solution.py
@@ -116,7 +116,10 @@
     conv_blocks = conv_out.reshape(images, local_groups, -1)
     out_mean = lax.psum(jnp.sum(conv_blocks, 2), ("band", "chan")) / pixel_count
     deviation = conv_blocks - out_mean[:, :, None]
-    out_var = lax.psum(jnp.sum(deviation * deviation, 2), ("band", "chan")) / pixel_count
+    out_var = (
+        jnp.sum(lax.all_gather(jnp.sum(deviation * deviation, 2), ("band", "chan")), axis=0)
+        / pixel_count
+    )
     activated = jnp.maximum(
         apply_norm(conv_blocks, out_mean, out_var, conv_out.shape, full_gain, full_shift), 0.0
     ).astype(jnp.bfloat16)

time: 356 us -> 381 us (1.070)
  blocking collectives: 166 us -> 191 us
    all_gather x0 -> x1, blocking collectives: none -> 66.1 us  [per_device(): lax.all_gather(jnp.sum(deviation * deviation, 2), ('band', 'chan'))]
    psum x1 -> x0, blocking collectives: 40.9 us -> none  [per_device(): lax.psum(jnp.sum(deviation * deviation, 2), ('band', 'chan')) / pixel_count]
where the time goes in v1:
time: 381 us; the launch traced here: 380 us
  blocking collectives  191 us (50%)
  waiting for transfers between devices  75.2 us (20%)
  matrix products  41.1 us (11%)
  local copies, waits for them, and re-layouts  27.1 us (7%)
  other arithmetic  21.6 us (6%)
  between operations  13.7 us (4%)
  starting transfers between devices  11 us (3%)
    all_gather x1, blocking collectives, per_device(): lax.all_gather(jnp.sum(deviation * deviation, 2), ('band', 'chan'))  66.1 us
    psum x1, blocking collectives, per_device(): out_mean = lax.psum(jnp.sum(conv_blocks, 2), ('band', 'chan')) / pixel_count  37 us
    all_to_all x1, waiting for transfers between devices, per_device(): lax.all_to_all(joined, 'chan', split_axis=2, concat_axis=1, tiled=True)  37 us
    psum x1, blocking collectives, per_device(): lat_mean = lax.psum(jnp.sum(lat_blocks, 2), 'band') / pixel_count  33.2 us
    dot_general x9, matrix products, conv_taps(): jnp.einsum('oc,ncrw->norw', taps_weight[row_tap, col_tap], window, prefer...  32.1 us
    psum x1, blocking collectives, per_device(): lat_var = lax.psum(jnp.sum(deviation * deviation, 2), 'band') / pixel_count  29.5 us
    all_gather x1, waiting for transfers between devices, per_device(): lax.all_gather(fine_features, 'chan', axis=1, tiled=True)  23.6 us
    ppermute x2, waiting for transfers between devices, extended_2(): lax.ppermute(head, axis, [((i + 1) % count, i) for i in range(ends)])  13.9 us
  transfers between devices with their start and end apart: 7, of which 4 were waited for; matrix products, arithmetic and copies ran while one was open for 7% of the time, Pallas kernels for 0%

profile of v1, /device:TPU:0, one launch (start us, length us, event | category | flops | bytes accessed | tf_op | source)
XLA Modules:
  0.0 380.4 jit_solution(7835147488105375304)
XLA Ops:
  6.6 3.1 copy.21
  9.8 0.4 fusion.60
  10.1 2.4 collective-permute-start
  12.6 1.3 collective-permute-start.1
  13.9 4.2 %collective-permute-done.1 = bf16[2,128,1,256]{3,2,1,0:T(2,128)(2,1)S(1)} collective-permute-done((bf16[2,128,1,256]{3,2,1,0:T(2,128)(2,1)S(1)}, bf16[2,128,1,256]{3,2,1,0:T(2,128)(2,1)S(1)}, u32[]{:S(2)}, u32[]{:S(2)}) %collective-permute-start.1) | collective-permute-done | bytes 131104 | tf_op jit(solution)/shard_map/ppermute | solution.py:21
  18.1 0.8 broadcast_select_fusion.1
  18.9 0.8 maximum_convert_fusion.6
  19.7 0.3 fusion.59
  20.1 1.1 pad_maximum_fusion.1
  21.2 1.0 fusion.43
  22.2 2.4 pad_maximum_fusion.2
  24.6 3.2 copy.22
  27.9 0.6 fusion.32
  28.5 0.3 pad_maximum_fusion
  28.8 5.2 %copy.23 = f32[2,128,8,256,2]{1,4,3,2,0:T(2,128)} copy(f32[2,128,8,256,2]{1,3,2,0,4:T(8,128)S(1)} %pad_maximum_fusion) | data formatting | bytes 8388608 | tf_op jit(solution)/shard_map/stack | solution.py:35
  34.0 23.6 %all-gather.8.cloned.1.call-done = bf16[2,192,8,512]{3,1,2,0:T(8,128)(2,1)} async-done(((bf16[2,96,8,512]{3,1,2,0:T(8,128)(2,1)}), bf16[2,192,8,512]{3,1,2,0:T(8,128)(2,1)}) %all-gather.8.cloned.1.call-update) | async-done | bytes 3145744 | tf_op jit(solution)/shard_map/all_gather | solution.py:87
  57.5 5.4 %bitcast_reduce_fusion.1 = (f32[2,128]{1,0:T(2,128)S(1)}, f32[2,8,512,128]{3,2,1,0:T(8,128)}) fusion(bf16[2,192,8,512]{3,1,2,0:T(8,128)(2,1)} %all-gather.8.cloned.1.call-done, bf16[128,192]{0,1:T(8,128)(2,1)S(1)} %copy-done.5), kind=kOutput, calls=%fused_computation.7 | convolution fusion | flops 403701504 | bytes 7390208 | tf_op jit(solution)/shard_map/oc,ncrw->norw/dot_general | solution.py:84
  62.9 0.1 reduce_sum.66
  63.0 0.1 reduce_sum.67
  63.1 33.2 %psum.21 = f32[2,16]{1,0:T(2,128)S(1)} all-reduce(f32[2,16]{1,0:T(2,128)S(1)} %reduce_sum.67), channel_id=1, replica_groups=mesh['band'=16,'chan'=2] {'band'}, use_global_device_ids=true, to_apply=%region_2.0 | all-reduce | flops 32 | bytes 256 | tf_op jit(solution)/shard_map/psum | solution.py:91
  96.4 0.1 sub.53
  96.5 2.8 multiply_reduce_fusion.1
  99.3 0.1 reduce_sum.73
  99.4 29.5 %psum.22 = f32[2,16]{1,0:T(2,128)S(1)} all-reduce(f32[2,16]{1,0:T(2,128)S(1)} %reduce_sum.73), channel_id=1, replica_groups=mesh['band'=16,'chan'=2] {'band'}, use_global_device_ids=true, to_apply=%region_5.6 | all-reduce | flops 32 | bytes 256 | tf_op jit(solution)/shard_map/psum | solution.py:93
  128.9 0.1 mul.72
  129.0 4.3 %add_convert_fusion.1 = bf16[2,128,8,512]{1,3,2,0:T(8,128)(2,1)S(1)} fusion(f32[2,128,8,512]{1,3,2,0:T(8,128)} %bitcast.139, f32[2,8,512,128]{3,2,1,0:T(8,128)} %get-tuple-element.18, f32[128]{0:T(128)S(1)} %convert_element_type.33, f32[128]{0:T(128)S(1)} %convert_element_type.32, f32[2,128]{1,0:T(2,128)S(1)} %mul.72, f32[2,128]{1,0:T(2,128)S(1)} %sub.53), kind=kLoop, calls=%fused_computation.12 | loop fusion | flops 6291456 | bytes 10488832 | tf_op jit(solution)/shard_map/convert_element_type | solution.py:102
  133.4 1.5 copy.24
  134.9 3.8 all-to-all-start
  138.7 0.7 all-gather.10.cloned.1.call-update
  139.4 37.0 %all-to-all-done = bf16[2,128,8,512]{1,3,0,2:T(8,128)(2,1)S(1)} async-done(((bf16[2,128,8,512]{1,3,0,2:T(8,128)(2,1)}), bf16[2,128,8,512]{1,3,0,2:T(8,128)(2,1)S(1)}, u32[]{:S(2)}, u32[]{:S(2)}) %all-to-all-start) | async-done | bytes 2097184 | tf_op jit(solution)/shard_map/all_to_all | solution.py:103
  176.4 3.5 copy.42
  179.9 3.2 all_to_all.16
  183.1 1.1 fusion.58
  184.2 2.2 collective-permute-start.2
  186.4 11.5 %all-gather.2 = bf16[2,1,128]{2,1,0:T(2,128)(2,1)S(1)} all-gather(bf16[1,1,128]{2,1,0:T(2,128)(2,1)S(1)} %bitcast.146), channel_id=1, replica_groups=mesh['band'=16,'chan'=2] {'chan'}, dimensions={0}, use_global_device_ids=true | all-gather | bytes 768 | tf_op jit(solution)/shard_map/all_gather | solution.py:106
  198.0 4.2 %all-gather.3 = bf16[2,1,128]{2,1,0:T(2,128)(2,1)S(1)} all-gather(bf16[1,1,128]{2,1,0:T(2,128)(2,1)S(1)} %bitcast.147), channel_id=1, replica_groups=mesh['band'=16,'chan'=2] {'chan'}, dimensions={0}, use_global_device_ids=true | all-gather | bytes 768 | tf_op jit(solution)/shard_map/all_gather | solution.py:107
  202.2 4.2 %all-gather.4 = bf16[2,1,128]{2,1,0:T(2,128)(2,1)S(1)} all-gather(bf16[1,1,128]{2,1,0:T(2,128)(2,1)S(1)} %bitcast.148), channel_id=1, replica_groups=mesh['band'=16,'chan'=2] {'chan'}, dimensions={0}, use_global_device_ids=true | all-gather | bytes 768 | tf_op jit(solution)/shard_map/all_gather | solution.py:109
  206.4 4.9 %all_gather.30 = bf16[256,256]{1,0:T(8,128)(2,1)S(1)} all-gather(bf16[128,256]{1,0:T(8,128)(2,1)S(1)} %copy-done.4), channel_id=1, replica_groups=mesh['band'=16,'chan'=2] {'chan'}, dimensions={0}, use_global_device_ids=true | all-gather | bytes 196608 | tf_op jit(solution)/shard_map/all_gather | solution.py:108
  211.4 1.3 collective-permute-start.3
  212.7 1.7 fusion.44
  214.5 2.7 fusion.7
  217.2 9.8 %collective-permute-done.3 = bf16[2,256,1,512]{1,3,2,0:T(8,128)(2,1)S(1)} collective-permute-done((bf16[2,256,1,512]{1,3,2,0:T(8,128)(2,1)}, bf16[2,256,1,512]{1,3,2,0:T(8,128)(2,1)S(1)}, u32[]{:S(2)}, u32[]{:S(2)}) %collective-permute-start.3) | collective-permute-done | bytes 524320 | tf_op jit(solution)/shard_map/ppermute | solution.py:21
  226.9 1.0 fusion.6
  227.9 2.7 fusion.11
  230.6 2.7 fusion.19
  233.3 2.7 fusion.21
  236.0 2.7 fusion.23
  238.7 2.7 fusion.25
  241.5 2.8 fusion.27
  244.2 0.7 copy-done.1
  244.9 11.3 %bitcast_reduce_fusion = (f32[2,256]{1,0:T(2,128)S(1)}, f32[2,4,512,256]{3,2,1,0:T(8,128)}) fusion(bf16[3,3,256,256]{3,2,1,0:T(8,128)(2,1)} %all-gather.10.cloned.1.call-done, bf16[2,256,6,514]{1,3,2,0:T(8,128)(2,1)S(1)} %fusion.6, f32[2,4,512,256]{3,2,1,0:T(8,128)} %fusion.11, f32[2,4,512,256]{3,2,1,0:T(8,128)} %fusion.19, f32[2,4,512,256]{3,2,1,0:T(8,128)} %fusion.21, ...), kind=kOutput, calls=%fused_computation.5 | convolution fusion | flops 546307584 | bytes 39979008 | tf_op jit(solution)/shard_map/oc,ncrw->norw/dot_general | solution.py:46
  256.2 0.1 reduce_sum.89
  256.3 0.1 reduce_sum.90
  256.4 37.0 %psum.23 = f32[2,32]{1,0:T(2,128)S(1)} all-reduce(f32[2,32]{1,0:T(2,128)S(1)} %reduce_sum.90), channel_id=1, replica_groups=mesh['band'=16,'chan'=2] {'band','chan'}, use_global_device_ids=true, to_apply=%region_8.9 | all-reduce | flops 64 | bytes 512 | tf_op jit(solution)/shard_map/psum | solution.py:117
  293.5 0.1 sub.57
  293.6 2.7 multiply_reduce_fusion
  296.2 0.1 reduce_sum.92
  296.3 0.1 reduce_sum.93
  296.4 66.1 %all-gather.1 = f32[32,2,32]{2,1,0:T(2,128)S(1)} all-gather(f32[1,2,32]{2,1,0:T(2,128)S(1)} %bitcast.142), channel_id=2, replica_groups=mesh['band'=16,'chan'=2] {'band','chan'}, dimensions={0}, use_global_device_ids=true | all-gather | bytes 8448 | tf_op jit(solution)/shard_map/all_gather | solution.py:120
  362.6 0.1 mul.85
  362.7 3.7 fusion.33
  366.4 2.9 exponential_reduce_fusion
  369.3 0.4 log_subtract_fusion
  369.8 3.8 %copy.27 = f32[2,200,4,512]{3,2,1,0:T(4,128)} copy(f32[2,200,4,512]{3,1,2,0:T(8,128)S(1)} %log_subtract_fusion) | data formatting | bytes 6553600 | tf_op jit(solution)/shard_map/sub | solution.py:131
  (42 shorter events, 0.6 us)
Async XLA Ops:
  6.5 356.2 %copy-start = (bf16[200,256]{1,0:T(8,128)(2,1)S(1)}, bf16[200,256]{1,0:T(8,128)(2,1)}, u32[]{:S(2)}) copy-start(bf16[200,256]{1,0:T(8,128)(2,1)} %param.21) | copy-start | bytes 307204
  6.5 3.2 copy-start.2
  6.5 7.3 %copy-start.6 = (bf16[128]{0:T(256)(128)(2,1)S(1)}, bf16[128]{0:T(256)(128)(2,1)}, u32[]{:S(2)}) copy-start(bf16[128]{0:T(256)(128)(2,1)} %param.14) | copy-start | bytes 772
  6.5 7.3 %copy-start.7 = (bf16[128]{0:T(256)(128)(2,1)S(1)}, bf16[128]{0:T(256)(128)(2,1)}, u32[]{:S(2)}) copy-start(bf16[128]{0:T(256)(128)(2,1)} %param.15) | copy-start | bytes 772
  6.5 51.0 %all-gather.8.cloned.1.call-start = ((), (), s32[]{:S(2)}) async-start(), calls=%async_computation.1 | async-start | bytes 4718592 | tf_op jit(solution)/shard_map/all_gather | solution.py:87
  10.1 3.8 collective-permute-start
  12.6 5.5 %collective-permute-start.1 = (bf16[2,128,1,256]{3,2,1,0:T(2,128)(2,1)S(1)}, bf16[2,128,1,256]{3,2,1,0:T(2,128)(2,1)S(1)}, u32[]{:S(2)}, u32[]{:S(2)}) collective-permute-start(bf16[2,128,1,256]{3,2,1,0:T(2,128)(2,1)S(1)} %get-tuple-element.16), channel_id=1, source_target_pairs={{2,0},{4,2},{6,4},{8,6},{10,8},{12,10},{14,12},{16,14},{18,16},{20... | collective-permute-start | bytes 393224 | tf_op jit(solution)/shard_map/ppermute | solution.py:21
  28.8 28.8 %copy-start.5 = (bf16[128,192]{0,1:T(8,128)(2,1)S(1)}, bf16[128,192]{0,1:T(8,128)(2,1)}, u32[]{:S(2)}) copy-start(bf16[128,192]{0,1:T(8,128)(2,1)} %param.13) | copy-start | bytes 147460
  134.9 41.5 %all-to-all-start = ((bf16[2,128,8,512]{1,3,0,2:T(8,128)(2,1)}), bf16[2,128,8,512]{1,3,0,2:T(8,128)(2,1)S(1)}, u32[]{:S(2)}, u32[]{:S(2)}) async-start(bf16[2,128,8,512]{1,3,0,2:T(8,128)(2,1)} %copy.24), calls=%async_computation | async-start | bytes 4194304 | tf_op jit(solution)/shard_map/all_to_all | solution.py:103
  138.6 74.0 %all-gather.10.cloned.1.call-start = ((), (), s32[]{:S(2)}) async-start(), calls=%async_computation.2 | async-start | bytes 1769472 | tf_op jit(solution)/shard_map/all_gather | solution.py:105
  179.9 6.5 %copy-start.8 = (bf16[128]{0:T(256)(128)(2,1)S(1)}, bf16[128]{0:T(256)(128)(2,1)}, u32[]{:S(2)}) copy-start(bf16[128]{0:T(256)(128)(2,1)} %param.17) | copy-start | bytes 772
  179.9 18.1 %copy-start.9 = (bf16[128]{0:T(256)(128)(2,1)S(1)}, bf16[128]{0:T(256)(128)(2,1)}, u32[]{:S(2)}) copy-start(bf16[128]{0:T(256)(128)(2,1)} %param.18) | copy-start | bytes 772
  179.9 22.3 %copy-start.10 = (bf16[128]{0:T(256)(128)(2,1)S(1)}, bf16[128]{0:T(256)(128)(2,1)}, u32[]{:S(2)}) copy-start(bf16[128]{0:T(256)(128)(2,1)} %param.20) | copy-start | bytes 772
  179.9 26.6 %copy-start.4 = (bf16[128,256]{1,0:T(8,128)(2,1)S(1)}, bf16[128,256]{1,0:T(8,128)(2,1)}, u32[]{:S(2)}) copy-start(bf16[128,256]{1,0:T(8,128)(2,1)} %param.19) | copy-start | bytes 196612
  184.2 30.2 %collective-permute-start.2 = (bf16[2,256,1,512]{1,3,2,0:T(8,128)(2,1)}, bf16[2,256,1,512]{1,3,2,0:T(8,128)(2,1)S(1)}, u32[]{:S(2)}, u32[]{:S(2)}) collective-permute-start(bf16[2,256,1,512]{1,3,2,0:T(8,128)(2,1)} %get-tuple-element.9), channel_id=1, source_target_pairs={{0,1},{1,2},{2,3},{3,4},{4,5},{5,6},{6,7},{7,8},{8,9},{9,10},{10,1... | collective-permute-start | bytes 1572872 | tf_op jit(solution)/shard_map/ppermute | solution.py:19
  211.4 15.6 %collective-permute-start.3 = (bf16[2,256,1,512]{1,3,2,0:T(8,128)(2,1)}, bf16[2,256,1,512]{1,3,2,0:T(8,128)(2,1)S(1)}, u32[]{:S(2)}, u32[]{:S(2)}) collective-permute-start(bf16[2,256,1,512]{1,3,2,0:T(8,128)(2,1)} %get-tuple-element.10), channel_id=1, source_target_pairs={{1,0},{2,1},{3,2},{4,3},{5,4},{6,5},{7,6},{8,7},{9,8},{10,9},{11,1... | collective-permute-start | bytes 1572872 | tf_op jit(solution)/shard_map/ppermute | solution.py:21
  212.7 1.8 copy-start.3
  241.5 3.4 copy-start.1
Sparse Core Ops, SparseCore 0:
  9.9 47.6 all-gather.7
  141.0 33.2 all-gather.9
